TPU v7x, 8 devices: a whole 2x2x1 slice. The times are simulated.
8 devices in a mesh: dp: 2 (over z, y), sp: 4 (over x, core).
Axes of the slice: x: 2, y: 2, z: 1, core: 2. Of those that a mesh axis runs over, the one named last changes fastest.
Arguments:
- hidden: bfloat16 [16, 1536, 3072], P('dp', 'sp'), parts along dimension 0
- cond_vec: bfloat16 [16, 3072], P('dp'), parts along dimension 0
- pos_ids: int32 [1536, 3], P('sp')
- w_mod: bfloat16 [2, 3072, 9216], replicated
- b_mod: bfloat16 [2, 9216], replicated
- w_in: bfloat16 [2, 3072, 21504], replicated
- b_in: bfloat16 [2, 21504], replicated
- q_gain: bfloat16 [2, 128], replicated
- k_gain: bfloat16 [2, 128], replicated
- w_out: bfloat16 [2, 15360, 3072], replicated
- b_out: bfloat16 [2, 3072], replicated
Outputs:
- output: bfloat16 [16, 1536, 3072], P('dp', 'sp'), parts along dimension 0
There are 2 independent parts. A program takes and returns all parts, laid end to end along the dimension named above; an argument that names none is the same for every part.
All inputs are finite; a program needn't handle non-finite values.
Results may differ from a plain program's by a relative error of at most 0.0114649.
Values are sent between devices in bfloat16 or wider.
A program may use at most 2.5 GiB of HBM per device.

v0:
```python
import math
import jax
import jax.numpy as jnp
from jax import lax
from jax.sharding import PartitionSpec as P

HEAD = 128
ROPE_SPLIT = (16, 56, 56)
ROPE_THETA = 10000.0
NORM_EPS = 1e-6
Q_BLOCK = 256


def rope_tables(pos_ids):
    angle_parts = []
    for column, rope_dim in enumerate(ROPE_SPLIT):
        inv_freq = 1.0 / (ROPE_THETA ** (jnp.arange(0, rope_dim, 2, dtype=jnp.float32) / rope_dim))
        angle_parts.append(pos_ids[:, column:column + 1].astype(jnp.float32) * inv_freq)
    angles = jnp.concatenate(angle_parts, axis=1)
    return jnp.cos(angles), jnp.sin(angles)


def rms_norm(tensor, gain):
    sq_mean = jnp.mean(tensor * tensor, axis=-1, keepdims=True)
    return tensor * lax.rsqrt(sq_mean + NORM_EPS) * gain.astype(jnp.float32)


def apply_rope(tensor, cos_t, sin_t):
    paired = tensor.reshape(tensor.shape[:-1] + (tensor.shape[-1] // 2, 2))
    even_v = paired[..., 0]
    odd_v = paired[..., 1]
    cos_b = cos_t[None, :, None, :]
    sin_b = sin_t[None, :, None, :]
    rotated = jnp.stack([even_v * cos_b - odd_v * sin_b, even_v * sin_b + odd_v * cos_b], axis=-1)
    return rotated.reshape(tensor.shape)


def modulation(cond_vec, w_mod, b_mod):
    mod_act = jax.nn.silu(cond_vec.astype(jnp.float32)).astype(jnp.bfloat16)
    mod_vals = jnp.dot(mod_act, w_mod, preferred_element_type=jnp.float32) + b_mod.astype(jnp.float32)
    mod_vals = mod_vals.astype(jnp.bfloat16).astype(jnp.float32)
    return jnp.split(mod_vals[:, None, :], 3, axis=-1)


def project_in(hidden, mod_shift, mod_scale, w_in, b_in):
    x_float = hidden.astype(jnp.float32)
    centered = x_float - jnp.mean(x_float, axis=-1, keepdims=True)
    normed = centered * lax.rsqrt(jnp.mean(centered * centered, axis=-1, keepdims=True) + NORM_EPS)
    modded = ((1.0 + mod_scale) * normed + mod_shift).astype(jnp.bfloat16)
    proj_f = jnp.einsum('bsd,dn->bsn', modded, w_in, preferred_element_type=jnp.float32)
    return (proj_f + b_in.astype(jnp.float32)).astype(jnp.bfloat16)


def qkv_heads(proj_in, model_dim, q_gain, k_gain, cos_t, sin_t):
    head_shape = proj_in.shape[:2] + (model_dim // HEAD, HEAD)
    q_raw = proj_in[..., :model_dim].reshape(head_shape).astype(jnp.float32)
    k_raw = proj_in[..., model_dim:2 * model_dim].reshape(head_shape).astype(jnp.float32)
    v_heads = proj_in[..., 2 * model_dim:3 * model_dim].reshape(head_shape)
    q_heads = apply_rope(rms_norm(q_raw, q_gain), cos_t, sin_t).astype(jnp.bfloat16)
    k_heads = apply_rope(rms_norm(k_raw, k_gain), cos_t, sin_t).astype(jnp.bfloat16)
    return q_heads, k_heads, v_heads


def local_attention(queries, keys_all, values_all):
    n_batch, q_rows, n_heads, head_dim = queries.shape
    q_block = math.gcd(q_rows, Q_BLOCK)
    score_scale = head_dim ** -0.5

    def per_block(blk_idx):
        q_blk = lax.dynamic_slice_in_dim(queries, blk_idx * q_block, q_block, axis=1)
        scores = jnp.einsum('bqhd,bkhd->bhqk', q_blk, keys_all, preferred_element_type=jnp.float32) * score_scale
        row_max = jnp.max(scores, axis=-1, keepdims=True)
        weights = jnp.exp(scores - row_max)
        row_sum = jnp.sum(weights, axis=-1)
        attn_blk = jnp.einsum('bhqk,bkhd->bqhd', weights.astype(jnp.bfloat16), values_all, preferred_element_type=jnp.float32)
        return (attn_blk / jnp.swapaxes(row_sum, 1, 2)[..., None]).astype(jnp.bfloat16)

    blocks_out = lax.map(per_block, jnp.arange(q_rows // q_block))
    return jnp.moveaxis(blocks_out, 0, 1).reshape(n_batch, q_rows, n_heads, head_dim)


def project_out(hidden, attn_out, mlp_in, mod_gate, w_out, b_out):
    model_dim = attn_out.shape[-1]
    mlp_act = jax.nn.gelu(mlp_in.astype(jnp.float32), approximate=True).astype(jnp.bfloat16)
    out_f = jnp.einsum('bsd,dn->bsn', attn_out, w_out[:model_dim], preferred_element_type=jnp.float32)
    out_f = out_f + jnp.einsum('bsm,mn->bsn', mlp_act, w_out[model_dim:], preferred_element_type=jnp.float32)
    block_out = (out_f + b_out.astype(jnp.float32)).astype(jnp.bfloat16)
    return (hidden.astype(jnp.float32) + mod_gate * block_out.astype(jnp.float32)).astype(jnp.bfloat16)


def solution(mesh):
    row_spec = P('dp', 'sp', None)
    replicated = P()

    def local_forward(hidden, cond_vec, pos_ids, w_mod, b_mod, w_in, b_in, q_gain, k_gain, w_out, b_out):
        cos_t, sin_t = rope_tables(pos_ids)
        n_batch, local_rows, model_dim = hidden.shape
        for layer_idx in range(w_mod.shape[0]):
            mod_shift, mod_scale, mod_gate = modulation(cond_vec, w_mod[layer_idx], b_mod[layer_idx])
            proj_in = project_in(hidden, mod_shift, mod_scale, w_in[layer_idx], b_in[layer_idx])
            q_heads, k_heads, v_heads = qkv_heads(proj_in, model_dim, q_gain[layer_idx], k_gain[layer_idx], cos_t, sin_t)
            q_seq = lax.all_to_all(q_heads, 'sp', 2, 1, tiled=True)
            k_seq = lax.all_to_all(k_heads, 'sp', 2, 1, tiled=True)
            v_seq = lax.all_to_all(v_heads, 'sp', 2, 1, tiled=True)
            attn_seq = local_attention(q_seq, k_seq, v_seq)
            attn_rows = lax.all_to_all(attn_seq, 'sp', 1, 2, tiled=True).reshape(n_batch, local_rows, model_dim)
            hidden = project_out(hidden, attn_rows, proj_in[..., 3 * model_dim:], mod_gate, w_out[layer_idx], b_out[layer_idx])
        return hidden

    in_specs = (row_spec, P('dp', None), P('sp', None), replicated, replicated, replicated, replicated, replicated, replicated, replicated, replicated)
    return jax.shard_map(local_forward, mesh=mesh, in_specs=in_specs, out_specs=row_spec, check_vma=False)
```

profile of v0, /device:TPU:0, one launch (start us, length us, event | category | flops | bytes accessed | tf_op | source)
XLA Modules:
  0.0 4929.4 jit_solution(16746674348371071812)
XLA Ops:
  38.6 426.6 %add_convert_fusion.1 = bf16[8,384,21504]{2,1,0:T(8,128)(2,1)} fusion(f32[21504]{0:T(1024)S(1)} %bitcast.270, bf16[2,3072,21504]{2,1,0:T(8,128)(2,1)} %param.20, bf16[8,384,3072]{2,1,0:T(8,128)(2,1)} %param.15, f32[8,3072]{1,0:T(8,128)S(1)} %get-tuple-element.128, f32[8,384]{1,0:T(8,128)S(1)} %add_rsqrt_fusion.5, ...), kind=kOutput, calls=%fused_computation.37 | convolution fusion | flops 406063153152 | bytes 283422720 | tf_op jit(solution)/shard_map/bsd,dn->bsn/dot_general | solution.py:50
  465.1 46.1 slice_bitcast_fusion.1
  525.9 36.1 fusion.131
  671.4 37.2 copy.147
  708.7 37.2 copy.140
  796.6 36.0 subtract_convert_fusion.2
  873.3 188.7 %all-to-all-done.1 = bf16[8,384,24,128]{1,3,0,2:T(8,128)(2,1)} async-done(((bf16[8,384,24,128]{1,3,0,2:T(8,128)(2,1)}), bf16[8,384,24,128]{1,3,0,2:T(8,128)(2,1)}, u32[]{:S(2)}, u32[]{:S(2)}) %all-to-all-start.1) | async-done | bytes 18874400 | tf_op jit(solution)/shard_map/all_to_all | solution.py:103
  1112.9 161.6 %all-to-all-done = bf16[8,384,24,128]{1,3,0,2:T(8,128)(2,1)} async-done(((bf16[8,384,24,128]{1,3,0,2:T(8,128)(2,1)}), bf16[8,384,24,128]{1,3,0,2:T(8,128)(2,1)}, u32[]{:S(2)}, u32[]{:S(2)}) %all-to-all-start) | async-done | bytes 18874400 | tf_op jit(solution)/shard_map/all_to_all | solution.py:102
  1306.2 552.8 %while.20 = (s32[]{:T(128)}, bf16[6,8,256,6,128]{4,2,0,3,1:T(8,128)(2,1)}, s32[6]{0:T(128)S(1)}, bf16[8,1536,6,128]{3,1,2,0:T(8,128)(2,1)}, bf16[8,1536,6,128]{3...) while((s32[]{:T(128)}, ...), condition=%wide.region_7.8_spmd, body=%wide.region_4.7_spmd.sunk | while | flops 9817792512 | bytes 270778496 | solution.py:78
  1910.1 182.4 %all-to-all-done.3 = bf16[8,1536,6,128]{3,0,2,1:T(8,128)(2,1)} async-done(((bf16[8,1536,6,128]{3,0,2,1:T(8,128)(2,1)}), bf16[8,1536,6,128]{3,0,2,1:T(8,128)(2,1)}, u32[]{:S(2)}, u32[]{:S(2)}) %all-to-all-start.3) | async-done | bytes 18874400 | tf_op jit(solution)/shard_map/all_to_all | solution.py:106
  2118.1 68.4 %fusion.86 = f32[8,384,3072]{2,1,0:T(8,128)} fusion(bf16[8,384,3072]{1,2,0:T(8,128)(2,1)} %bitcast.263, bf16[2,15360,3072]{2,1,0:T(8,128)(2,1)} %param.24), kind=kOutput, calls=%fused_computation.118 | convolution fusion | flops 57982058496 | bytes 75497472 | tf_op jit(solution)/shard_map/bsd,dn->bsn/dot_general | solution.py:85
  2186.5 305.1 %convert_reduce_fusion = (f32[8,384]{1,0:T(8,128)S(1)}, bf16[8,384,3072]{2,1,0:T(8,128)(2,1)}) fusion(f32[3072]{0:T(1024)S(1)} %bitcast.272, f32[8,384,3072]{2,1,0:T(8,128)} %fusion.86, bf16[2,15360,3072]{2,1,0:T(8,128)(2,1)} %param.24, bf16[8,384,21504]{2,1,0:T(8,128)(2,1)} %add_convert_fusion.1, f32[8,3072]{1,0:T(8,128)S(1)} %copy-done.13, ...), kind=kOutput, calls=%fused_computation.76 | convolution fusion | flops 232400093184 | bytes 226615296 | tf_op jit(solution)/shard_map/bsm,mn->bsn/dot_general | solution.py:86
  2500.4 427.0 %add_convert_fusion = bf16[8,384,21504]{2,1,0:T(8,128)(2,1)} fusion(f32[21504]{0:T(1024)S(1)} %bitcast.269, bf16[2,3072,21504]{2,1,0:T(8,128)(2,1)} %param.20, bf16[8,384,3072]{2,1,0:T(8,128)(2,1)} %get-tuple-element.145, f32[8,3072]{1,0:T(8,128)S(1)} %copy-done.15, f32[8,384]{1,0:T(8,128)S(1)} %add_rsqrt_fusion.4, ...), kind=kOutput, calls=%fused_computation.32 | convolution fusion | flops 406063153152 | bytes 283422720 | tf_op jit(solution)/shard_map/bsd,dn->bsn/dot_general | solution.py:50
  2927.5 46.1 slice_bitcast_fusion
  2988.2 36.1 fusion.133
  3132.1 37.2 copy.169
  3169.4 37.2 copy.162
  3256.1 35.6 subtract_convert_fusion
  3332.3 187.7 %all-to-all-done.5 = bf16[8,384,24,128]{1,3,0,2:T(8,128)(2,1)} async-done(((bf16[8,384,24,128]{1,3,0,2:T(8,128)(2,1)}), bf16[8,384,24,128]{1,3,0,2:T(8,128)(2,1)}, u32[]{:S(2)}, u32[]{:S(2)}) %all-to-all-start.5) | async-done | bytes 18874400 | tf_op jit(solution)/shard_map/all_to_all | solution.py:103
  3571.1 161.6 %all-to-all-done.4 = bf16[8,384,24,128]{1,3,0,2:T(8,128)(2,1)} async-done(((bf16[8,384,24,128]{1,3,0,2:T(8,128)(2,1)}), bf16[8,384,24,128]{1,3,0,2:T(8,128)(2,1)}, u32[]{:S(2)}, u32[]{:S(2)}) %all-to-all-start.4) | async-done | bytes 18874400 | tf_op jit(solution)/shard_map/all_to_all | solution.py:102
  3764.4 552.6 %while.21 = (s32[]{:T(128)}, bf16[6,8,256,6,128]{4,2,0,3,1:T(8,128)(2,1)}, s32[6]{0:T(128)S(1)}, bf16[8,1536,6,128]{3,1,2,0:T(8,128)(2,1)}, bf16[8,1536,6,128]{3...) while((s32[]{:T(128)}, ...), condition=%wide.region_15.16_spmd, body=%wide.region_12.15_spmd.sunk | while | flops 9817792512 | bytes 270778496 | solution.py:78
  4333.5 210.3 %all_to_all.138 = bf16[8,1536,6,128]{3,0,2,1:T(8,128)(2,1)} all-to-all(bf16[8,1536,6,128]{3,0,2,1:T(8,128)(2,1)S(1)} %copy.180), channel_id=1, replica_groups=mesh['dp'=2,'sp'=4] {'sp'}, dimensions={1} | all-to-all | bytes 37748736 | tf_op jit(solution)/shard_map/all_to_all | solution.py:106
  4568.1 68.6 %fusion.84 = f32[8,384,3072]{2,1,0:T(8,128)} fusion(bf16[8,384,3072]{1,2,0:T(8,128)(2,1)} %bitcast.264, bf16[2,15360,3072]{2,1,0:T(8,128)(2,1)} %param.24), kind=kOutput, calls=%fused_computation.116 | convolution fusion | flops 57982058496 | bytes 75497472 | tf_op jit(solution)/shard_map/bsd,dn->bsn/dot_general | solution.py:85
  4636.7 292.5 %fusion.81 = bf16[8,384,3072]{2,1,0:T(8,128)(2,1)} fusion(bf16[8,384,3072]{2,1,0:T(8,128)(2,1)} %get-tuple-element.145, f32[8,384,3072]{2,1,0:T(8,128)} %fusion.84, f32[3072]{0:T(1024)S(1)} %bitcast.271, f32[8,3072]{1,0:T(8,128)S(1)} %copy-done.14, bf16[2,15360,3072]{2,1,0:T(8,128)(2,1)} %param.24, bf16[8,384,21504]{2,1,0:T(8,128)(2,1)} %add_convert_fusion), kind=kOutput, calls=%fused_computation.93 | convolution fusion | flops 232381218816 | bytes 226603008 | tf_op jit(solution)/shard_map/bsm,mn->bsn/dot_general | solution.py:86
  (180 shorter events, 1855.5 us)
Async XLA Ops:
  518.6 329.8 %all-to-all-start.2 = ((bf16[8,384,24,128]{3,1,0,2:T(8,128)(2,1)}), bf16[8,384,24,128]{3,1,0,2:T(8,128)(2,1)}, u32[]{:S(2)}, u32[]{:S(2)}) async-start(bf16[8,384,24,128]{3,1,0,2:T(8,128)(2,1)} %bitcast.250), calls=%async_computation.2 | async-start | bytes 37748736 | tf_op jit(solution)/shard_map/all_to_all | solution.py:104
  525.9 36.1 copy-start.23
  525.9 36.1 copy-start.24
  708.7 37.3 copy-start.20
  747.1 49.5 %copy-start.2 = (f32[384,64]{0,1:T(8,128)}, f32[384,64]{0,1:T(8,128)S(1)}, u32[]{:S(2)}) copy-start(f32[384,64]{0,1:T(8,128)S(1)} %get-tuple-element.134) | copy-start | bytes 294916
  747.1 35.9 copy-start
  848.4 213.6 %all-to-all-start.1 = ((bf16[8,384,24,128]{1,3,0,2:T(8,128)(2,1)}), bf16[8,384,24,128]{1,3,0,2:T(8,128)(2,1)}, u32[]{:S(2)}, u32[]{:S(2)}) async-start(bf16[8,384,24,128]{1,3,0,2:T(8,128)(2,1)} %copy.151), calls=%async_computation.1 | async-start | bytes 37748736 | tf_op jit(solution)/shard_map/all_to_all | solution.py:103
  1062.0 212.5 %all-to-all-start = ((bf16[8,384,24,128]{1,3,0,2:T(8,128)(2,1)}), bf16[8,384,24,128]{1,3,0,2:T(8,128)(2,1)}, u32[]{:S(2)}, u32[]{:S(2)}) async-start(bf16[8,384,24,128]{1,3,0,2:T(8,128)(2,1)} %copy.144), calls=%async_computation | async-start | bytes 37748736 | tf_op jit(solution)/shard_map/all_to_all | solution.py:102
  1859.0 29.9 copy-start.18
  1859.0 30.5 copy-start.8
  1859.0 30.5 copy-start.9
  1879.8 212.7 %all-to-all-start.3 = ((bf16[8,1536,6,128]{3,0,2,1:T(8,128)(2,1)}), bf16[8,1536,6,128]{3,0,2,1:T(8,128)(2,1)}, u32[]{:S(2)}, u32[]{:S(2)}) async-start(bf16[8,1536,6,128]{3,0,2,1:T(8,128)(2,1)} %copy.158), calls=%async_computation.3 | async-start | bytes 37748736 | tf_op jit(solution)/shard_map/all_to_all | solution.py:106
  2118.1 68.4 %copy-start.13 = (f32[8,3072]{1,0:T(8,128)S(1)}, f32[8,3072]{1,0:T(8,128)}, u32[]{:S(2)}) copy-start(f32[8,3072]{1,0:T(8,128)} %get-tuple-element.127) | copy-start | bytes 294916
  2186.5 313.9 %copy-start.15 = (f32[8,3072]{1,0:T(8,128)S(1)}, f32[8,3072]{1,0:T(8,128)}, u32[]{:S(2)}) copy-start(f32[8,3072]{1,0:T(8,128)} %get-tuple-element.125) | copy-start | bytes 294916
  2186.5 313.9 %copy-start.16 = (f32[8,3072]{1,0:T(8,128)S(1)}, f32[8,3072]{1,0:T(8,128)}, u32[]{:S(2)}) copy-start(f32[8,3072]{1,0:T(8,128)} %get-tuple-element.126) | copy-start | bytes 294916
  2186.5 313.9 %copy-start.17 = (f32[1,21504]{1,0:T(1,128)S(1)}, f32[1,21504]{1,0:T(1,128)}, u32[]{:S(2)}) copy-start(f32[1,21504]{1,0:T(1,128)} %get-tuple-element.136) | copy-start | bytes 258052
  2980.6 326.8 %all-to-all-start.6 = ((bf16[8,384,24,128]{3,1,0,2:T(8,128)(2,1)}), bf16[8,384,24,128]{3,1,0,2:T(8,128)(2,1)}, u32[]{:S(2)}, u32[]{:S(2)}) async-start(bf16[8,384,24,128]{3,1,0,2:T(8,128)(2,1)} %bitcast.251), calls=%async_computation.6 | async-start | bytes 37748736 | tf_op jit(solution)/shard_map/all_to_all | solution.py:104
  3169.4 37.2 copy-start.12
  3206.6 35.8 copy-start.1
  3206.6 35.8 copy-start.11
  3307.4 212.5 %all-to-all-start.5 = ((bf16[8,384,24,128]{1,3,0,2:T(8,128)(2,1)}), bf16[8,384,24,128]{1,3,0,2:T(8,128)(2,1)}, u32[]{:S(2)}, u32[]{:S(2)}) async-start(bf16[8,384,24,128]{1,3,0,2:T(8,128)(2,1)} %copy.173), calls=%async_computation.5 | async-start | bytes 37748736 | tf_op jit(solution)/shard_map/all_to_all | solution.py:103
  3520.0 212.7 %all-to-all-start.4 = ((bf16[8,384,24,128]{1,3,0,2:T(8,128)(2,1)}), bf16[8,384,24,128]{1,3,0,2:T(8,128)(2,1)}, u32[]{:S(2)}, u32[]{:S(2)}) async-start(bf16[8,384,24,128]{1,3,0,2:T(8,128)(2,1)} %copy.166), calls=%async_computation.4 | async-start | bytes 37748736 | tf_op jit(solution)/shard_map/all_to_all | solution.py:102
  4568.1 68.6 %copy-start.14 = (f32[8,3072]{1,0:T(8,128)S(1)}, f32[8,3072]{1,0:T(8,128)}, u32[]{:S(2)}) copy-start(f32[8,3072]{1,0:T(8,128)} %get-tuple-element.124) | copy-start | bytes 294916
  4568.1 68.6 %copy-start.19 = (f32[1,3072]{1,0:T(1,128)S(1)}, f32[1,3072]{1,0:T(1,128)}, u32[]{:S(2)}) copy-start(f32[1,3072]{1,0:T(1,128)} %get-tuple-element.140) | copy-start | bytes 36868
  (8 other events, 150.2 us)
where the time goes:
time: 4950 us; the launch traced here: 4930 us
  matrix products  2430 us (49%)
  waiting for transfers between devices  882 us (18%)
  other arithmetic  764 us (15%)
  local copies, waits for them, and re-layouts  584 us (12%)
  blocking collectives  210 us (4%)
  starting transfers between devices  52 us (1%)
    dot_general x2, matrix products, project_in(): jnp.einsum('bsd,dn->bsn', modded, w_in, preferred_element_type=jnp.float32)  854 us
    dot_general x2, matrix products, project_out(): jnp.einsum('bsm,mn->bsn', mlp_act, w_out[model_dim:], preferred_element_t...  598 us
    dot_general x12, matrix products, per_block(): jnp.einsum('bhqk,bkhd->bqhd', weights.astype(jnp.bfloat16), values_all, p...  404 us
    dot_general x12, matrix products, per_block(): jnp.einsum('bqhd,bkhd->bhqk', q_blk, keys_all, preferred_element_type=jnp...  396 us
    all_to_all x2, waiting for transfers between devices, local_forward(): k_seq = lax.all_to_all(k_heads, 'sp', 2, 1, tiled=True)  376 us
    all_to_all x2, waiting for transfers between devices, local_forward(): q_seq = lax.all_to_all(q_heads, 'sp', 2, 1, tiled=True)  323 us
    reduce_sum x12, other arithmetic, per_block(): row_sum = jnp.sum(weights, axis=-1)  290 us
    all_to_all x1, blocking collectives, local_forward(): lax.all_to_all(attn_seq, 'sp', 1, 2, tiled=True)  210 us
  transfers between devices with their start and end apart: 7, of which 5 were waited for; matrix products, arithmetic and copies ran while one was open for 16% of the time, Pallas kernels for 0%

commit v1 on v0

v1 whole, which is shorter than its diff:
```python
import functools
import math
import jax
import jax.numpy as jnp
from jax import lax
from jax.experimental import pallas as pl
from jax.experimental.pallas import tpu as pltpu
from jax.sharding import PartitionSpec as P

HEAD = 128
ROPE_SPLIT = (16, 56, 56)
ROPE_THETA = 10000.0
NORM_EPS = 1e-6
MIB = 1024 * 1024
LN_ROWS = 16


def rope_tables(pos):
    parts = []
    for column, rope_dim in enumerate(ROPE_SPLIT):
        inv_freq = 1.0 / (ROPE_THETA ** (jnp.arange(0, rope_dim, 2, dtype=jnp.float32) / rope_dim))
        parts.append(pos[..., column:column + 1].astype(jnp.float32) * jnp.repeat(inv_freq, 2))
    angles = jnp.concatenate(parts, axis=-1)
    sign = jnp.where(jnp.arange(HEAD) % 2 == 0, -1.0, 1.0)
    return jnp.cos(angles), jnp.sin(angles) * sign


def mod_kernel(me_ref, c_ref, w_ref, b_ref, o_ref):
    act = jax.nn.silu(c_ref[...].astype(jnp.float32)).astype(jnp.bfloat16)
    vals = jnp.dot(act, w_ref[0], preferred_element_type=jnp.float32) + b_ref[0].astype(jnp.float32)
    o_ref[0] = vals.astype(jnp.bfloat16)


def modulation(cond_vec, w_mod, b_mod, me, n_shard):
    n_layer, dim, width = w_mod.shape
    n_item = cond_vec.shape[0]
    share = width // n_shard
    cols = share // 2
    return pl.pallas_call(
        mod_kernel,
        grid_spec=pltpu.PrefetchScalarGridSpec(
            num_scalar_prefetch=1,
            grid=(n_layer, 2),
            in_specs=[
                pl.BlockSpec((n_item, dim), lambda l, j, me: (0, 0)),
                pl.BlockSpec((1, dim, cols), lambda l, j, me: (l, 0, me[0] * 2 + j)),
                pl.BlockSpec((1, 1, cols), lambda l, j, me: (l, 0, me[0] * 2 + j)),
            ],
            out_specs=pl.BlockSpec((1, n_item, cols), lambda l, j, me: (l, 0, j)),
        ),
        out_shape=jax.ShapeDtypeStruct((n_layer, n_item, share), jnp.bfloat16),
        compiler_params=pltpu.CompilerParams(vmem_limit_bytes=48 * MIB),
        name="modulation",
    )(me, cond_vec, w_mod, b_mod)


def proj_in_kernel(x_ref, mod_ref, w_ref, b_ref, gain_ref, cos_ref, sin_ref, *rest, n_qk, n_v, sub, cols):
    out_ref, u_ref, acc_ref = rest[-3:]
    j = pl.program_id(1)
    _, n_item, rows, dim = x_ref.shape
    width = w_ref.shape[2]

    @pl.when(j == 0)
    def _():
        for t in range(n_item):
            shift = mod_ref[t, :, :dim]
            scale = 1.0 + mod_ref[t, :, dim:2 * dim]

            def norm_step(i, carry):
                r = pl.ds(pl.multiple_of(i * LN_ROWS, LN_ROWS), LN_ROWS)
                x = x_ref[0, t, r, :].astype(jnp.float32)
                x = x - jnp.mean(x, axis=-1, keepdims=True)
                x = x * lax.rsqrt(jnp.mean(x * x, axis=-1, keepdims=True) + NORM_EPS)
                u_ref[t, r, :] = (scale * x + shift).astype(jnp.bfloat16)
                return carry

            lax.fori_loop(0, rows // LN_ROWS, norm_step, 0)

    def pieces(finish):
        waiting = None
        slot = 0
        for t in range(n_item):
            for s in range(rows // sub):
                for n in range(width // cols):
                    r = slice(s * sub, (s + 1) * sub)
                    acc_ref[slot] = jnp.dot(u_ref[t, r, :], w_ref[0, :, n * cols:(n + 1) * cols], preferred_element_type=jnp.float32)
                    if waiting is not None:
                        finish(*waiting)
                    waiting = (slot, t, r, n * cols)
                    slot = 1 - slot
        finish(*waiting)

    def biased(slot, c0):
        return (acc_ref[slot] + b_ref[0, :, c0:c0 + cols].astype(jnp.float32)).astype(jnp.bfloat16)

    @pl.when(j < 2 * n_qk)
    def _():
        gain = jnp.where(j < n_qk, gain_ref[0], gain_ref[1])
        even = lax.broadcasted_iota(jnp.int32, (sub, HEAD), 1) % 2 == 0

        def finish(slot, t, r, c0):
            h = biased(slot, c0).astype(jnp.float32)
            for d in range(0, cols, HEAD):
                v = h[:, d:d + HEAD]
                v = v * lax.rsqrt(jnp.mean(v * v, axis=-1, keepdims=True) + NORM_EPS) * gain
                swapped = jnp.where(even, pltpu.roll(v, HEAD - 1, 1), pltpu.roll(v, 1, 1))
                out_ref[0, t, r, c0 + d:c0 + d + HEAD] = (v * cos_ref[0, r, :] + swapped * sin_ref[0, r, :]).astype(jnp.bfloat16)

        pieces(finish)

    @pl.when((j >= 2 * n_qk) & (j < 2 * n_qk + n_v))
    def _():
        def finish(slot, t, r, c0):
            out_ref[0, t, r, c0:c0 + cols] = biased(slot, c0)

        pieces(finish)

    @pl.when(j >= 2 * n_qk + n_v)
    def _():
        def finish(slot, t, r, c0):
            h = biased(slot, c0).astype(jnp.float32)
            out_ref[0, t, r, c0:c0 + cols] = jax.nn.gelu(h, approximate=True).astype(jnp.bfloat16)

        pieces(finish)


def proj_in(x, mod, w_in, b_in, gain, cos, sin, layer, n_chunk, first=0, prev=None, block=1536, sub=192, cols=512):
    count, n_item, rows, dim = x.shape
    width = w_in.shape[2]
    in_specs = [
        pl.BlockSpec((1, n_item, rows, dim), lambda r, j: (r, 0, 0, 0)),
        pl.BlockSpec((n_item, 1, 3 * dim), lambda r, j: (0, 0, 0)),
        pl.BlockSpec((1, dim, block), lambda r, j: (layer, 0, j)),
        pl.BlockSpec((1, 1, block), lambda r, j: (layer, 0, j)),
        pl.BlockSpec((2, 1, HEAD), lambda r, j: (0, 0, 0)),
        pl.BlockSpec((1, rows, HEAD), lambda r, j: (first + r, 0, 0)),
        pl.BlockSpec((1, rows, HEAD), lambda r, j: (first + r, 0, 0)),
    ]
    operands = [x, mod, w_in, b_in, gain, cos, sin]
    aliases = {}
    if prev is not None:
        in_specs.append(pl.BlockSpec(memory_space=pl.ANY))
        operands.append(prev)
        aliases = {7: 0}
    return pl.pallas_call(
        functools.partial(proj_in_kernel, n_qk=dim // block, n_v=dim // block, sub=sub, cols=cols),
        grid=(count, width // block),
        in_specs=in_specs,
        out_specs=pl.BlockSpec((1, n_item, rows, block), lambda r, j: (first + r, 0, 0, j)),
        out_shape=jax.ShapeDtypeStruct((n_chunk, n_item, rows, width), jnp.bfloat16),
        scratch_shapes=[pltpu.VMEM((n_item, rows, dim), jnp.bfloat16), pltpu.VMEM((2, sub, cols), jnp.float32)],
        input_output_aliases=aliases,
        compiler_params=pltpu.CompilerParams(vmem_limit_bytes=60 * MIB),
        cost_estimate=pl.CostEstimate(flops=2 * count * n_item * rows * dim * width, bytes_accessed=2 * count * (dim * width + n_item * rows * width), transcendentals=0),
        name="proj_in",
    )(*operands)


def attention_kernel(q_ref, k_ref, v_ref, o_ref, s_ref, *, n_head, sub):
    n_chunk, _, rows, _ = q_ref.shape
    keys = n_chunk * rows
    exp_scale = HEAD ** -0.5 * math.log2(math.e)
    work = [(slice(h * HEAD, (h + 1) * HEAD), c, slice(s * sub, (s + 1) * sub)) for h in range(n_head) for c in range(n_chunk) for s in range(rows // sub)]

    def score(i):
        head, c, r = work[i]
        k = k_ref[:, 0, :, head].reshape(keys, HEAD)
        s_ref[i % 2] = lax.dot_general(q_ref[c, 0, r, head], k, (((1,), (1,)), ((), ())), preferred_element_type=jnp.float32)

    score(0)
    for i, (head, c, r) in enumerate(work):
        if i + 1 < len(work):
            score(i + 1)
        s = s_ref[i % 2]
        p = jnp.exp2((s - jnp.max(s, axis=-1, keepdims=True)) * exp_scale)
        total = jnp.sum(p, axis=-1, keepdims=True)
        v = v_ref[:, 0, :, head].reshape(keys, HEAD)
        o = jnp.dot(p.astype(jnp.bfloat16), v, preferred_element_type=jnp.float32)
        o_ref[c, 0, r, head] = (o / total).astype(jnp.bfloat16)


def attention(h, dim, n_head=4, sub=384):
    n_chunk, n_item, rows, _ = h.shape
    w = n_head * HEAD
    nb = dim // w
    block = (n_chunk, 1, rows, w)
    keys = n_chunk * rows
    return pl.pallas_call(
        functools.partial(attention_kernel, n_head=n_head, sub=sub),
        grid=(n_item, nb),
        in_specs=[
            pl.BlockSpec(block, lambda t, g: (0, t, 0, g)),
            pl.BlockSpec(block, lambda t, g: (0, t, 0, nb + g)),
            pl.BlockSpec(block, lambda t, g: (0, t, 0, 2 * nb + g)),
        ],
        out_specs=pl.BlockSpec(block, lambda t, g: (0, t, 0, g)),
        out_shape=jax.ShapeDtypeStruct((n_chunk, n_item, rows, dim), jnp.bfloat16),
        scratch_shapes=[pltpu.VMEM((2, sub, keys), jnp.float32)],
        compiler_params=pltpu.CompilerParams(vmem_limit_bytes=60 * MIB),
        cost_estimate=pl.CostEstimate(flops=4 * n_item * keys * keys * dim, bytes_accessed=8 * n_item * keys * dim, transcendentals=n_item * keys * keys * dim // HEAD),
        name="attention",
    )(h, h, h)


def proj_out_kernel(slot_ref, o_ref, g_ref, w_ref, b_ref, x_ref, mod_ref, *rest, k_attn, sub, cols):
    out_ref, acc_ref = rest[-2:]
    k = pl.program_id(1)
    last = pl.num_programs(1) - 1
    n_item, rows, dim = acc_ref.shape
    tiles = [(t, slice(s * sub, (s + 1) * sub), slice(n * cols, (n + 1) * cols)) for t in range(n_item) for s in range(rows // sub) for n in range(dim // cols)]

    def product(src, t, r, c):
        return jnp.dot(src[0, t, r, :], w_ref[0, :, c], preferred_element_type=jnp.float32)

    @pl.when(k == 0)
    def _():
        for t, r, c in tiles:
            acc_ref[t, r, c] = product(o_ref, t, r, c)

    @pl.when((k > 0) & (k < k_attn))
    def _():
        for t, r, c in tiles:
            acc_ref[t, r, c] += product(o_ref, t, r, c)

    @pl.when((k >= k_attn) & (k < last))
    def _():
        for t, r, c in tiles:
            acc_ref[t, r, c] += product(g_ref, t, r, c)

    @pl.when(k == last)
    def _():
        for t, r, c in tiles:
            y = acc_ref[t, r, c] + product(g_ref, t, r, c) + b_ref[0, :, c].astype(jnp.float32)
            gate = mod_ref[t, :, 2 * dim + c.start:2 * dim + c.stop]
            y = gate * y.astype(jnp.bfloat16).astype(jnp.float32)
            out_ref[0, t, r, c] = (x_ref[0, t, r, c].astype(jnp.float32) + y).astype(jnp.bfloat16)


def proj_out(o, h, w_out, b_out, x, mod, layer, slot, out_slots, first=0, x_first=0, count=None, prev=None, k_block=1536, sub=384, cols=512):
    n_chunk, n_item, rows, dim = o.shape
    depth = w_out.shape[1]
    k_attn = dim // k_block
    g_off = 3 * dim // k_block - k_attn
    in_specs = [
        pl.BlockSpec((1, n_item, rows, k_block), lambda r, k, sl: (first + r, 0, 0, jnp.minimum(k, k_attn - 1))),
        pl.BlockSpec((1, n_item, rows, k_block), lambda r, k, sl: (first + r, 0, 0, g_off + jnp.maximum(k, k_attn))),
        pl.BlockSpec((1, k_block, dim), lambda r, k, sl: (layer, k, 0)),
        pl.BlockSpec((1, 1, dim), lambda r, k, sl: (layer, 0, 0)),
        pl.BlockSpec((1, n_item, rows, dim), lambda r, k, sl: (x_first + r, 0, 0, 0)),
        pl.BlockSpec((n_item, 1, 3 * dim), lambda r, k, sl: (0, 0, 0)),
    ]
    operands = [slot, o, h, w_out, b_out, x, mod]
    aliases = {}
    if prev is not None:
        in_specs.append(pl.BlockSpec(memory_space=pl.ANY))
        operands.append(prev)
        aliases = {7: 0}
    return pl.pallas_call(
        functools.partial(proj_out_kernel, k_attn=k_attn, sub=sub, cols=cols),
        grid_spec=pltpu.PrefetchScalarGridSpec(
            num_scalar_prefetch=1,
            grid=(count, depth // k_block),
            in_specs=in_specs,
            out_specs=pl.BlockSpec((1, n_item, rows, dim), lambda r, k, sl: (sl[0] + r, 0, 0, 0)),
            scratch_shapes=[pltpu.VMEM((n_item, rows, dim), jnp.float32)],
        ),
        out_shape=jax.ShapeDtypeStruct((out_slots, n_item, rows, dim), jnp.bfloat16),
        input_output_aliases=aliases,
        compiler_params=pltpu.CompilerParams(vmem_limit_bytes=62 * MIB),
        cost_estimate=pl.CostEstimate(flops=2 * count * n_item * rows * dim * depth, bytes_accessed=2 * count * dim * depth, transcendentals=0),
        name="proj_out",
    )(*operands)


def solution(mesh):
    row_spec = P('dp', 'sp', None)
    n_shard = mesh.shape['sp']

    def local_forward(hidden, cond_vec, pos_ids, w_mod, b_mod, w_in, b_in, q_gain, k_gain, w_out, b_out):
        n_batch, rows, dim = hidden.shape
        n_item = n_batch // n_shard
        me = lax.axis_index('sp')
        to = lambda rel: [(i, i ^ rel) for i in range(n_shard)]
        by_owner = hidden.reshape(n_shard, n_item, rows, dim)

        def share(rel):
            return lax.dynamic_slice_in_dim(by_owner, me ^ rel, 1, axis=0)

        got = [share(0)] + [lax.ppermute(share(rel), 'sp', to(rel)) for rel in range(1, n_shard)]

        me_arr = me.astype(jnp.int32).reshape(1)
        mod_share = modulation(cond_vec, w_mod, b_mod[:, None, :], me_arr, n_shard)
        mod_all = lax.all_gather(mod_share, 'sp', axis=2, tiled=True)
        mod_mine = lax.dynamic_slice_in_dim(mod_all, me * n_item, n_item, axis=1).astype(jnp.float32)[:, :, None, :]
        pos_all = lax.all_gather(pos_ids, 'sp', axis=0, tiled=False)
        cos, sin = rope_tables(pos_all[me ^ jnp.arange(n_shard)])
        gains = jnp.stack([q_gain, k_gain], axis=1).astype(jnp.float32)[:, :, None, :]
        b_in3 = b_in[:, None, :]
        b_out3 = b_out[:, None, :]
        zero = jnp.zeros((1,), jnp.int32)
        half = n_shard // 2

        near = jnp.concatenate(got[:half], axis=0)
        far = jnp.concatenate(got[half:], axis=0)
        h = proj_in(near, mod_mine[0], w_in, b_in3, gains[0], cos, sin, 0, n_shard)
        h = proj_in(far, mod_mine[0], w_in, b_in3, gains[0], cos, sin, 0, n_shard, first=half, prev=h)
        o = attention(h, dim)
        x = proj_out(o, h, w_out, b_out3, near, mod_mine[0], 0, zero, n_shard, count=half)
        x = proj_out(o, h, w_out, b_out3, far, mod_mine[0], 0, zero + half, n_shard, first=half, count=half, prev=x)

        h = proj_in(x, mod_mine[1], w_in, b_in3, gains[1], cos, sin, 1, n_shard)
        o = attention(h, dim)
        sent = {}
        for rel in (2, 3, 1):
            y = proj_out(o, h, w_out, b_out3, x, mod_mine[1], 1, zero, 1, first=rel, x_first=rel, count=1)
            sent[rel] = lax.ppermute(y, 'sp', to(rel))
        out = proj_out(o, h, w_out, b_out3, x, mod_mine[1], 1, me_arr, n_shard, first=0, x_first=0, count=1)
        for rel in (1, 2, 3):
            out = lax.dynamic_update_slice_in_dim(out, sent[rel], me ^ rel, axis=0)
        return out.reshape(n_batch, rows, dim)

    in_specs = (row_spec, P('dp', None), P('sp', None)) + (P(),) * 8
    return jax.shard_map(local_forward, mesh=mesh, in_specs=in_specs, out_specs=row_spec, check_vma=False)
```

time: 4950 us -> 2440 us (0.49)
  matrix products: 2430 us -> 0 us
  Pallas kernels: 0 us -> 2050 us
  waiting for transfers between devices: 882 us -> 113 us
  other arithmetic: 764 us -> 13.1 us
  local copies, waits for them, and re-layouts: 584 us -> 42.1 us
    dot_general x32 -> x0, matrix products: 2430 us -> none  [the longest x2 854 us: project_in(): jnp.einsum('bsd,dn->bsn', modded, w_in, preferred_element_type=jnp.float32)]
    pallas_call x0 -> x12, Pallas kernels: none -> 2050 us  [the longest x3 1020 us: proj_in(): pl.pallas_call(functools.partial(proj_in_kernel, n_qk=dim // block, n_v=d...]
    all_to_all x7 -> x0, waiting for transfers between devices: 882 us -> none  [the longest x2 376 us: local_forward(): k_seq = lax.all_to_all(k_heads, 'sp', 2, 1, tiled=True)]
    reduce_sum x19 -> x0, other arithmetic: 396 us -> none  [the longest x12 290 us: per_block(): row_sum = jnp.sum(weights, axis=-1)]
    all_gather x0 -> x2, blocking collectives: none -> 215 us  [the longest x1 207 us: local_forward(): pos_all = lax.all_gather(pos_ids, 'sp', axis=0, tiled=False)]
    all_to_all x1 -> x0, blocking collectives: 210 us -> none  [local_forward(): lax.all_to_all(attn_seq, 'sp', 1, 2, tiled=True)]
    all_to_all x8 -> x0, local copies, waits for them, and re-layouts: 186 us -> none  [the longest x2 49.9 us: local_forward(): lax.all_to_all(attn_seq, 'sp', 1, 2, tiled=True)]
    convert_element_type x12 -> x0, local copies, waits for them, and re-layouts: 180 us -> none  [the longest x2 74.5 us: qkv_heads(): q_raw = proj_in[..., :model_dim].reshape(head_shape).astype(jnp.float32)]
  transfers between devices with their start and end apart: 7 -> 6, of which waited for: 5 -> 1; matrix products, arithmetic and copies ran while one was open for 16% -> 1% of each run, Pallas kernels for 0% -> 14%
where the time goes in v1:
time: 2440 us
  Pallas kernels  2050 us (84%)
  blocking collectives  215 us (9%)
  waiting for transfers between devices  113 us (5%)
  local copies, waits for them, and re-layouts  42.1 us (2%)
    pallas_call x3, Pallas kernels, proj_in(): pl.pallas_call(functools.partial(proj_in_kernel, n_qk=dim // block, n_v=d...  1020 us
    pallas_call x6, Pallas kernels, proj_out(): pl.pallas_call(functools.partial(proj_out_kernel, k_attn=k_attn, sub=sub,...  732 us
    pallas_call x2, Pallas kernels, attention(): pl.pallas_call(functools.partial(attention_kernel, n_head=n_head, sub=sub...  281 us
    all_gather x1, blocking collectives, local_forward(): pos_all = lax.all_gather(pos_ids, 'sp', axis=0, tiled=False)  207 us
    ppermute x3, waiting for transfers between devices, local_forward(): sent[rel] = lax.ppermute(y, 'sp', to(rel))  113 us
  transfers between devices with their start and end apart: 6, of which 1 were waited for; matrix products, arithmetic and copies ran while one was open for 1% of the time, Pallas kernels for 14%

profile of v1, /device:TPU:0, one launch (start us, length us, event | category | flops | bytes accessed | tf_op | source)
XLA Modules:
  0.0 2437.2 jit_solution(3775716213001445651)
XLA Ops:
  0.0 14.1 constant_dynamic-slice_fusion.1
  15.0 2.5 collective-permute-start
  17.6 207.1 %all-gather = s32[1536,3]{0,1:T(4,128)S(1)} all-gather(s32[384,3]{0,1:T(4,128)S(1)} %copy-done.4), channel_id=2, replica_groups=mesh['dp'=2,'sp'=4] {'sp'}, dimensions={0}, use_global_device_ids=true | all-gather | bytes 23040 | tf_op jit(solution)/shard_map/all_gather | solution.py:295
  225.8 10.4 modulation.1
  237.8 7.9 all_gather.9
  247.1 4.0 sine_multiply_fusion
  252.0 8.2 pad_maximum_fusion.x_ref
  260.2 254.9 %proj_in.3.rest_0_ = bf16[4,2,384,21504]{3,2,1,0:T(8,128)(2,1)} custom-call(bf16[2,2,384,3072]{3,2,1,0:T(8,128)(2,1)} %pad_maximum_fusion.x_ref, f32[2,1,9216]{2,1,0:T(1,128)} %get-tuple-element.12.mod_ref, bf16[2,3072,21504]{2,1,0:T(8,128)(2,1)} %w_ref.15, bf16[2,1,21504]{2,1,0:T(2,128)(2,1)} %copy.23.b_ref, f32[2,1,128]{2,1,0:T(1,128)} %bitcast.33, ...), custom_call_target="tpu_custom_call" | custom-call | flops 202937204736 | bytes 330301440 | tf_op jit(solution)/shard_map/proj_in/pallas_call | solution.py:145
  515.1 4.8 constant_dynamic-update-slice_fusion.1
  519.9 4.8 constant_dynamic-update-slice_fusion.x_ref
  524.6 268.4 %proj_in.4.q_ref.k_ref.v_ref.g_ref = bf16[4,2,384,21504]{3,2,1,0:T(8,128)(2,1)} custom-call(bf16[2,2,384,3072]{3,2,1,0:T(8,128)(2,1)} %constant_dynamic-update-slice_fusion.x_ref, f32[2,1,9216]{2,1,0:T(1,128)} %get-tuple-element.12.mod_ref, bf16[2,3072,21504]{2,1,0:T(8,128)(2,1)} %w_ref.15, ...), custom_call_target="tpu_custom_call", output_to_operand_aliasing={{}: (7, {})} | custom-call | flops 202937204736 | bytes 330301440 | tf_op jit(solution)/shard_map/proj_in/pallas_call | solution.py:145
  793.1 140.6 %attention.2.o_ref = bf16[4,2,384,3072]{3,2,1,0:T(8,128)(2,1)} custom-call(bf16[4,2,384,21504]{3,2,1,0:T(8,128)(2,1)} %proj_in.4.q_ref.k_ref.v_ref.g_ref, bf16[4,2,384,21504]{3,2,1,0:T(8,128)(2,1)} %proj_in.4.q_ref.k_ref.v_ref.g_ref, bf16[4,2,384,21504]{3,2,1,0:T(8,128)(2,1)} %proj_in.4.q_ref.k_ref.v_ref.g_ref), custom_call_target="tpu_custom_call" | custom-call | flops 57982058496 | bytes 75497472 | tf_op jit(solution)/shard_map/attention/pallas_call | solution.py:188
  933.7 175.9 %proj_out.6.rest_0_ = bf16[4,2,384,3072]{3,2,1,0:T(8,128)(2,1)} custom-call(s32[1]{0:T(128)} %constant.53.clone.1.slot_ref, bf16[4,2,384,3072]{3,2,1,0:T(8,128)(2,1)} %attention.2.o_ref, bf16[4,2,384,21504]{3,2,1,0:T(8,128)(2,1)} %proj_in.4.q_ref.k_ref.v_ref.g_ref, bf16[2,15360,3072]{2,1,0:T(8,128)(2,1)} %w_ref.19, bf16[2,1,3072]{2,1,0:T(2,128)(2,1)} %copy.26.b_ref, ...), custom_call_target="tpu_custom_call" | custom-call | flops 144955146240 | bytes 188743680 | tf_op jit(solution)/shard_map/proj_out/pallas_call | solution.py:258
  1109.7 175.2 %proj_out.7.x_ref = bf16[4,2,384,3072]{3,2,1,0:T(8,128)(2,1)} custom-call(s32[1]{0:T(128)} %constant.15.clone.1.slot_ref, bf16[4,2,384,3072]{3,2,1,0:T(8,128)(2,1)} %attention.2.o_ref, bf16[4,2,384,21504]{3,2,1,0:T(8,128)(2,1)} %proj_in.4.q_ref.k_ref.v_ref.g_ref, bf16[2,15360,3072]{2,1,0:T(8,128)(2,1)} %w_ref.19, ...), custom_call_target="tpu_custom_call", output_to_operand_aliasing={{}: (7, {})} | custom-call | flops 144955146240 | bytes 188743680 | tf_op jit(solution)/shard_map/proj_out/pallas_call | solution.py:258
  1284.9 500.4 %proj_in.5.q_ref.k_ref.v_ref.g_ref = bf16[4,2,384,21504]{3,2,1,0:T(8,128)(2,1)} custom-call(bf16[4,2,384,3072]{3,2,1,0:T(8,128)(2,1)} %proj_out.7.x_ref, f32[2,1,9216]{2,1,0:T(1,128)} %get-tuple-element.11.mod_ref, bf16[2,3072,21504]{2,1,0:T(8,128)(2,1)} %w_ref.15, bf16[2,1,21504]{2,1,0:T(2,128)(2,1)} %copy.23.b_ref, f32[2,1,128]{2,1,0:T(1,128)} %bitcast.32, ...), custom_call_target="tpu_custom_call" | custom-call | flops 405874409472 | bytes 660602880 | tf_op jit(solution)/shard_map/proj_in/pallas_call | solution.py:145
  1785.3 140.7 %attention.3.o_ref = bf16[4,2,384,3072]{3,2,1,0:T(8,128)(2,1)} custom-call(bf16[4,2,384,21504]{3,2,1,0:T(8,128)(2,1)} %proj_in.5.q_ref.k_ref.v_ref.g_ref, bf16[4,2,384,21504]{3,2,1,0:T(8,128)(2,1)} %proj_in.5.q_ref.k_ref.v_ref.g_ref, bf16[4,2,384,21504]{3,2,1,0:T(8,128)(2,1)} %proj_in.5.q_ref.k_ref.v_ref.g_ref), custom_call_target="tpu_custom_call" | custom-call | flops 57982058496 | bytes 75497472 | tf_op jit(solution)/shard_map/attention/pallas_call | solution.py:188
  1926.0 85.4 %proj_out.11 = bf16[1,2,384,3072]{3,2,1,0:T(8,128)(2,1)} custom-call(s32[1]{0:T(128)} %constant.53.clone.1.slot_ref, bf16[4,2,384,3072]{3,2,1,0:T(8,128)(2,1)} %attention.3.o_ref, bf16[4,2,384,21504]{3,2,1,0:T(8,128)(2,1)} %proj_in.5.q_ref.k_ref.v_ref.g_ref, bf16[2,15360,3072]{2,1,0:T(8,128)(2,1)} %w_ref.19, bf16[2,1,3072]{2,1,0:T(2,128)(2,1)} %copy.26.b_ref, ...), custom_call_target="tpu_custom_call" | custom-call | flops 72477573120 | bytes 94371840 | tf_op jit(solution)/shard_map/proj_out/pallas_call | solution.py:258
  2011.3 98.4 %proj_out.10 = bf16[1,2,384,3072]{3,2,1,0:T(8,128)(2,1)} custom-call(s32[1]{0:T(128)} %constant.53.clone.1.slot_ref, bf16[4,2,384,3072]{3,2,1,0:T(8,128)(2,1)} %attention.3.o_ref, bf16[4,2,384,21504]{3,2,1,0:T(8,128)(2,1)} %proj_in.5.q_ref.k_ref.v_ref.g_ref, bf16[2,15360,3072]{2,1,0:T(8,128)(2,1)} %w_ref.19, bf16[2,1,3072]{2,1,0:T(2,128)(2,1)} %copy.26.b_ref, ...), custom_call_target="tpu_custom_call" | custom-call | flops 72477573120 | bytes 94371840 | tf_op jit(solution)/shard_map/proj_out/pallas_call | solution.py:258
  2109.7 112.3 %proj_out.9 = bf16[1,2,384,3072]{3,2,1,0:T(8,128)(2,1)} custom-call(s32[1]{0:T(128)} %constant.53.clone.1.slot_ref, bf16[4,2,384,3072]{3,2,1,0:T(8,128)(2,1)} %attention.3.o_ref, bf16[4,2,384,21504]{3,2,1,0:T(8,128)(2,1)} %proj_in.5.q_ref.k_ref.v_ref.g_ref, bf16[2,15360,3072]{2,1,0:T(8,128)(2,1)} %w_ref.19, bf16[2,1,3072]{2,1,0:T(2,128)(2,1)} %copy.26.b_ref, ...), custom_call_target="tpu_custom_call" | custom-call | flops 72477573120 | bytes 94371840 | tf_op jit(solution)/shard_map/proj_out/pallas_call | solution.py:258
  2224.0 85.2 %proj_out.8 = bf16[4,2,384,3072]{3,2,1,0:T(8,128)(2,1)} custom-call(s32[1]{0:T(128)} %bitcast.me_ref.slot_ref, bf16[4,2,384,3072]{3,2,1,0:T(8,128)(2,1)} %attention.3.o_ref, bf16[4,2,384,21504]{3,2,1,0:T(8,128)(2,1)} %proj_in.5.q_ref.k_ref.v_ref.g_ref, bf16[2,15360,3072]{2,1,0:T(8,128)(2,1)} %w_ref.19, bf16[2,1,3072]{2,1,0:T(2,128)(2,1)} %copy.26.b_ref, ...), custom_call_target="tpu_custom_call" | custom-call | flops 72477573120 | bytes 94371840 | tf_op jit(solution)/shard_map/proj_out/pallas_call | solution.py:258
  2309.2 4.8 constant_dynamic-update-slice_fusion.4
  2314.0 113.3 %collective-permute-done.4 = bf16[1,2,384,3072]{3,2,1,0:T(8,128)(2,1)} collective-permute-done((bf16[1,2,384,3072]{3,2,1,0:T(8,128)(2,1)}, bf16[1,2,384,3072]{3,2,1,0:T(8,128)(2,1)}, u32[]{:S(2)}, u32[]{:S(2)}) %collective-permute-start.4) | collective-permute-done | bytes 4718624 | tf_op jit(solution)/shard_map/ppermute | solution.py:316
  2427.3 4.8 constant_dynamic-update-slice_fusion.3
  2432.2 4.8 constant_dynamic-update-slice_fusion.2
  (49 shorter events, 7.6 us)
Async XLA Ops:
  0.0 17.6 copy-start.4
  0.0 225.7 %copy-start.2 = (bf16[2,9216]{1,0:T(2,128)(2,1)S(1)}, bf16[2,9216]{1,0:T(2,128)(2,1)}, u32[]{:S(2)}) copy-start(bf16[2,9216]{1,0:T(2,128)(2,1)} %param.15) | copy-start | bytes 110596
  0.0 225.8 %copy-start = (bf16[8,3072]{1,0:T(8,128)(2,1)S(1)}, bf16[8,3072]{1,0:T(8,128)(2,1)}, u32[]{:S(2)}) copy-start(bf16[8,3072]{1,0:T(8,128)(2,1)} %c_ref.1) | copy-start | bytes 147460
  14.1 237.8 %collective-permute-start.2 = (bf16[1,2,384,3072]{3,2,1,0:T(8,128)(2,1)}, bf16[1,2,384,3072]{3,2,1,0:T(8,128)(2,1)}, u32[]{:S(2)}, u32[]{:S(2)}) collective-permute-start(bf16[1,2,384,3072]{3,2,1,0:T(8,128)(2,1)} %get-tuple-element.6), channel_id=1, source_target_pairs={{0,1},{1,0},{2,3},{3,2},{4,5},{5,4},{6,7},{7,6}} | collective-permute-start | bytes 14155784 | tf_op jit(solution)/shard_map/ppermute | solution.py:289
  15.0 500.1 %collective-permute-start = (bf16[1,2,384,3072]{3,2,1,0:T(8,128)(2,1)}, bf16[1,2,384,3072]{3,2,1,0:T(8,128)(2,1)}, u32[]{:S(2)}, u32[]{:S(2)}) collective-permute-start(bf16[1,2,384,3072]{3,2,1,0:T(8,128)(2,1)} %get-tuple-element.8), channel_id=1, source_target_pairs={{0,2},{1,3},{2,0},{3,1},{4,6},{5,7},{6,4},{7,5}} | collective-permute-start | bytes 14155784 | tf_op jit(solution)/shard_map/ppermute | solution.py:289
  17.5 502.4 %collective-permute-start.1 = (bf16[1,2,384,3072]{3,2,1,0:T(8,128)(2,1)}, bf16[1,2,384,3072]{3,2,1,0:T(8,128)(2,1)}, u32[]{:S(2)}, u32[]{:S(2)}) collective-permute-start(bf16[1,2,384,3072]{3,2,1,0:T(8,128)(2,1)} %get-tuple-element.7), channel_id=1, source_target_pairs={{0,3},{1,2},{2,1},{3,0},{4,7},{5,6},{6,5},{7,4}} | collective-permute-start | bytes 14155784 | tf_op jit(solution)/shard_map/ppermute | solution.py:289
  225.8 10.5 copy-start.1
  225.8 11.3 copy-start.5
  225.8 11.3 copy-start.6
  225.8 11.3 copy-start.3
  2222.1 210.1 %collective-permute-start.5 = (bf16[1,2,384,3072]{3,2,1,0:T(8,128)(2,1)}, bf16[1,2,384,3072]{3,2,1,0:T(8,128)(2,1)}, u32[]{:S(2)}, u32[]{:S(2)}) collective-permute-start(bf16[1,2,384,3072]{3,2,1,0:T(8,128)(2,1)} %proj_out.11), channel_id=1, source_target_pairs={{0,3},{1,2},{2,1},{3,0},{4,7},{5,6},{6,5},{7,4}} | collective-permute-start | bytes 14155784 | tf_op jit(solution)/shard_map/ppermute | solution.py:316
  2222.1 205.2 %collective-permute-start.4 = (bf16[1,2,384,3072]{3,2,1,0:T(8,128)(2,1)}, bf16[1,2,384,3072]{3,2,1,0:T(8,128)(2,1)}, u32[]{:S(2)}, u32[]{:S(2)}) collective-permute-start(bf16[1,2,384,3072]{3,2,1,0:T(8,128)(2,1)} %proj_out.10), channel_id=1, source_target_pairs={{0,2},{1,3},{2,0},{3,1},{4,6},{5,7},{6,4},{7,5}} | collective-permute-start | bytes 14155784 | tf_op jit(solution)/shard_map/ppermute | solution.py:316
  2223.8 85.4 %collective-permute-start.3 = (bf16[1,2,384,3072]{3,2,1,0:T(8,128)(2,1)}, bf16[1,2,384,3072]{3,2,1,0:T(8,128)(2,1)}, u32[]{:S(2)}, u32[]{:S(2)}) collective-permute-start(bf16[1,2,384,3072]{3,2,1,0:T(8,128)(2,1)} %proj_out.9), channel_id=1, source_target_pairs={{0,1},{1,0},{2,3},{3,2},{4,5},{5,4},{6,7},{7,6}} | collective-permute-start | bytes 14155784 | tf_op jit(solution)/shard_map/ppermute | solution.py:316

commit v2 on v1

--- a/solution.py
+++ b/solution.py
@@ -60,44 +60,47 @@
     _, n_item, rows, dim = x_ref.shape
     width = w_ref.shape[2]
 
-    @pl.when(j == 0)
-    def _():
-        for t in range(n_item):
-            shift = mod_ref[t, :, :dim]
-            scale = 1.0 + mod_ref[t, :, dim:2 * dim]
-
-            def norm_step(i, carry):
-                r = pl.ds(pl.multiple_of(i * LN_ROWS, LN_ROWS), LN_ROWS)
-                x = x_ref[0, t, r, :].astype(jnp.float32)
-                x = x - jnp.mean(x, axis=-1, keepdims=True)
-                x = x * lax.rsqrt(jnp.mean(x * x, axis=-1, keepdims=True) + NORM_EPS)
-                u_ref[t, r, :] = (scale * x + shift).astype(jnp.bfloat16)
-                return carry
-
-            lax.fori_loop(0, rows // LN_ROWS, norm_step, 0)
-
-    def pieces(finish):
-        waiting = None
-        slot = 0
-        for t in range(n_item):
-            for s in range(rows // sub):
-                for n in range(width // cols):
-                    r = slice(s * sub, (s + 1) * sub)
-                    acc_ref[slot] = jnp.dot(u_ref[t, r, :], w_ref[0, :, n * cols:(n + 1) * cols], preferred_element_type=jnp.float32)
-                    if waiting is not None:
-                        finish(*waiting)
-                    waiting = (slot, t, r, n * cols)
-                    slot = 1 - slot
-        finish(*waiting)
+    parts = [slice(s * sub, (s + 1) * sub) for s in range(rows // sub)]
+
+    def norm(t, r):
+        shift = mod_ref[t, :, :dim]
+        scale = 1.0 + mod_ref[t, :, dim:2 * dim]
+        for i in range(r.start, r.stop, LN_ROWS):
+            x = x_ref[0, t, i:i + LN_ROWS, :].astype(jnp.float32)
+            x = x - jnp.mean(x, axis=-1, keepdims=True)
+            x = x * lax.rsqrt(jnp.mean(x * x, axis=-1, keepdims=True) + NORM_EPS)
+            u_ref[t, i:i + LN_ROWS, :] = (scale * x + shift).astype(jnp.bfloat16)
+
+    work = [(r, c0) for r in parts for c0 in range(0, width, cols)]
+    assert len(work) % 2 == 0
+
+    def pieces(finish, with_norm=False):
+        if with_norm:
+            norm(0, parts[0])
+
+        def step(t, carry):
+            waiting = (1, jnp.maximum(t - 1, 0)) + work[-1]
+            for i, (r, c0) in enumerate(work):
+                acc_ref[i % 2] = jnp.dot(u_ref[t, r, :], w_ref[0, :, c0:c0 + cols], preferred_element_type=jnp.float32)
+                finish(*waiting)
+                waiting = (i % 2, t, r, c0)
+                if with_norm and c0 == 0:
+                    p = parts.index(r) + 1
+                    if p < len(parts):
+                        norm(t, parts[p])
+                    else:
+                        norm(jnp.minimum(t + 1, n_item - 1), parts[0])
+            return carry
+
+        lax.fori_loop(0, n_item, step, 0)
+        finish(1, n_item - 1, *work[-1])
 
     def biased(slot, c0):
         return (acc_ref[slot] + b_ref[0, :, c0:c0 + cols].astype(jnp.float32)).astype(jnp.bfloat16)
 
-    @pl.when(j < 2 * n_qk)
-    def _():
-        gain = jnp.where(j < n_qk, gain_ref[0], gain_ref[1])
-        even = lax.broadcasted_iota(jnp.int32, (sub, HEAD), 1) % 2 == 0
-
+    even = lax.broadcasted_iota(jnp.int32, (sub, HEAD), 1) % 2 == 0
+
+    def rotate(gain):
         def finish(slot, t, r, c0):
             h = biased(slot, c0).astype(jnp.float32)
             for d in range(0, cols, HEAD):
@@ -106,7 +109,15 @@
                 swapped = jnp.where(even, pltpu.roll(v, HEAD - 1, 1), pltpu.roll(v, 1, 1))
                 out_ref[0, t, r, c0 + d:c0 + d + HEAD] = (v * cos_ref[0, r, :] + swapped * sin_ref[0, r, :]).astype(jnp.bfloat16)
 
-        pieces(finish)
+        return finish
+
+    @pl.when(j == 0)
+    def _():
+        pieces(rotate(gain_ref[0]), with_norm=True)
+
+    @pl.when((j > 0) & (j < 2 * n_qk))
+    def _():
+        pieces(rotate(jnp.where(j < n_qk, gain_ref[0], gain_ref[1])))
 
     @pl.when((j >= 2 * n_qk) & (j < 2 * n_qk + n_v))
     def _():
@@ -207,37 +218,53 @@
     k = pl.program_id(1)
     last = pl.num_programs(1) - 1
     n_item, rows, dim = acc_ref.shape
-    tiles = [(t, slice(s * sub, (s + 1) * sub), slice(n * cols, (n + 1) * cols)) for t in range(n_item) for s in range(rows // sub) for n in range(dim // cols)]
+    tiles = [(slice(s * sub, (s + 1) * sub), slice(n * cols, (n + 1) * cols)) for s in range(rows // sub) for n in range(dim // cols)]
+
+    def each_tile(fn):
+        def step(t, carry):
+            for r, c in tiles:
+                fn(t, r, c)
+            return carry
+
+        lax.fori_loop(0, n_item, step, 0)
 
     def product(src, t, r, c):
         return jnp.dot(src[0, t, r, :], w_ref[0, :, c], preferred_element_type=jnp.float32)
 
     @pl.when(k == 0)
     def _():
-        for t, r, c in tiles:
+        def fn(t, r, c):
             acc_ref[t, r, c] = product(o_ref, t, r, c)
 
+        each_tile(fn)
+
     @pl.when((k > 0) & (k < k_attn))
     def _():
-        for t, r, c in tiles:
+        def fn(t, r, c):
             acc_ref[t, r, c] += product(o_ref, t, r, c)
 
+        each_tile(fn)
+
     @pl.when((k >= k_attn) & (k < last))
     def _():
-        for t, r, c in tiles:
+        def fn(t, r, c):
             acc_ref[t, r, c] += product(g_ref, t, r, c)
 
+        each_tile(fn)
+
     @pl.when(k == last)
     def _():
-        for t, r, c in tiles:
+        def fn(t, r, c):
             y = acc_ref[t, r, c] + product(g_ref, t, r, c) + b_ref[0, :, c].astype(jnp.float32)
             gate = mod_ref[t, :, 2 * dim + c.start:2 * dim + c.stop]
             y = gate * y.astype(jnp.bfloat16).astype(jnp.float32)
             out_ref[0, t, r, c] = (x_ref[0, t, r, c].astype(jnp.float32) + y).astype(jnp.bfloat16)
 
+        each_tile(fn)
+
 
 def proj_out(o, h, w_out, b_out, x, mod, layer, slot, out_slots, first=0, x_first=0, count=None, prev=None, k_block=1536, sub=384, cols=512):
-    n_chunk, n_item, rows, dim = o.shape
+    _, n_item, rows, dim = o.shape
     depth = w_out.shape[1]
     k_attn = dim // k_block
     g_off = 3 * dim // k_block - k_attn
@@ -281,18 +308,17 @@
         n_item = n_batch // n_shard
         me = lax.axis_index('sp')
         to = lambda rel: [(i, i ^ rel) for i in range(n_shard)]
-        by_owner = hidden.reshape(n_shard, n_item, rows, dim)
-
-        def share(rel):
-            return lax.dynamic_slice_in_dim(by_owner, me ^ rel, 1, axis=0)
-
-        got = [share(0)] + [lax.ppermute(share(rel), 'sp', to(rel)) for rel in range(1, n_shard)]
-
         me_arr = me.astype(jnp.int32).reshape(1)
         mod_share = modulation(cond_vec, w_mod, b_mod[:, None, :], me_arr, n_shard)
         mod_all = lax.all_gather(mod_share, 'sp', axis=2, tiled=True)
+        pos_all = lax.all_gather(pos_ids, 'sp', axis=0, tiled=False)
+        by_owner, mod_all, pos_all = lax.optimization_barrier((hidden.reshape(n_shard, n_item, rows, dim), mod_all, pos_all))
+
+        def share(rel):
+            return lax.dynamic_slice_in_dim(by_owner, me ^ rel, 1, axis=0)
+
+        got = [share(0)] + [lax.ppermute(share(rel), 'sp', to(rel)) for rel in range(1, n_shard)]
         mod_mine = lax.dynamic_slice_in_dim(mod_all, me * n_item, n_item, axis=1).astype(jnp.float32)[:, :, None, :]
-        pos_all = lax.all_gather(pos_ids, 'sp', axis=0, tiled=False)
         cos, sin = rope_tables(pos_all[me ^ jnp.arange(n_shard)])
         gains = jnp.stack([q_gain, k_gain], axis=1).astype(jnp.float32)[:, :, None, :]
         b_in3 = b_in[:, None, :]

time: 2440 us -> 2150 us (0.88)
  blocking collectives: 215 us -> 17.8 us
  Pallas kernels: 2050 us -> 1950 us
    all_gather x1, blocking collectives: 207 us -> 6.9 us  [local_forward(): pos_all = lax.all_gather(pos_ids, 'sp', axis=0, tiled=False)]
    pallas_call x6, Pallas kernels: 732 us -> 681 us  [proj_out(): pl.pallas_call(functools.partial(proj_out_kernel, k_attn=k_attn, sub=sub,...]
    pallas_call x3, Pallas kernels: 1020 us -> 979 us  [proj_in(): pl.pallas_call(functools.partial(proj_in_kernel, n_qk=dim // block, n_v=d...]
  transfers between devices with their start and end apart: 6 -> 6, of which waited for: 1 -> 1; matrix products, arithmetic and copies ran while one was open for 1% -> 1% of each run, Pallas kernels for 14% -> 16%
where the time goes in v2:
time: 2150 us; the launch traced here: 2140 us
  Pallas kernels  1950 us (91%)
  waiting for transfers between devices  112 us (5%)
  local copies, waits for them, and re-layouts  43.6 us (2%)
    pallas_call x3, Pallas kernels, proj_in(): pl.pallas_call(functools.partial(proj_in_kernel, n_qk=dim // block, n_v=d...  979 us
    pallas_call x6, Pallas kernels, proj_out(): pl.pallas_call(functools.partial(proj_out_kernel, k_attn=k_attn, sub=sub,...  681 us
    pallas_call x2, Pallas kernels, attention(): pl.pallas_call(functools.partial(attention_kernel, n_head=n_head, sub=sub...  281 us
    ppermute x3, waiting for transfers between devices, local_forward(): sent[rel] = lax.ppermute(y, 'sp', to(rel))  112 us
  transfers between devices with their start and end apart: 6, of which 1 were waited for; matrix products, arithmetic and copies ran while one was open for 1% of the time, Pallas kernels for 16%

profile of v2, /device:TPU:0, one launch (start us, length us, event | category | flops | bytes accessed | tf_op | source)
XLA Modules:
  0.0 2142.2 jit_solution(9801791402936562943)
XLA Ops:
  1.6 10.4 modulation.1
  12.1 10.9 all_gather.9
  23.0 6.9 all-gather
  29.9 14.1 constant_dynamic-slice_fusion.1
  44.1 1.8 collective-permute-start
  49.8 4.0 sine_multiply_fusion
  54.6 8.2 pad_maximum_fusion.x_ref
  62.9 246.8 %proj_in.3.rest_0_ = bf16[4,2,384,21504]{3,2,1,0:T(8,128)(2,1)} custom-call(bf16[2,2,384,3072]{3,2,1,0:T(8,128)(2,1)} %pad_maximum_fusion.x_ref, f32[2,1,9216]{2,1,0:T(1,128)} %get-tuple-element.18.mod_ref, bf16[2,3072,21504]{2,1,0:T(8,128)(2,1)} %w_ref.15, bf16[2,1,21504]{2,1,0:T(2,128)(2,1)} %copy.23.b_ref, f32[2,1,128]{2,1,0:T(1,128)} %bitcast.33, ...), custom_call_target="tpu_custom_call" | custom-call | flops 202937204736 | bytes 330301440 | tf_op jit(solution)/shard_map/proj_in/pallas_call | solution.py:156
  309.7 4.8 constant_dynamic-update-slice_fusion.1
  314.5 4.8 constant_dynamic-update-slice_fusion.x_ref
  319.2 247.6 %proj_in.4.q_ref.k_ref.v_ref.g_ref = bf16[4,2,384,21504]{3,2,1,0:T(8,128)(2,1)} custom-call(bf16[2,2,384,3072]{3,2,1,0:T(8,128)(2,1)} %constant_dynamic-update-slice_fusion.x_ref, f32[2,1,9216]{2,1,0:T(1,128)} %get-tuple-element.18.mod_ref, bf16[2,3072,21504]{2,1,0:T(8,128)(2,1)} %w_ref.15, ...), custom_call_target="tpu_custom_call", output_to_operand_aliasing={{}: (7, {})} | custom-call | flops 202937204736 | bytes 330301440 | tf_op jit(solution)/shard_map/proj_in/pallas_call | solution.py:156
  566.9 140.5 %attention.2.o_ref = bf16[4,2,384,3072]{3,2,1,0:T(8,128)(2,1)} custom-call(bf16[4,2,384,21504]{3,2,1,0:T(8,128)(2,1)} %proj_in.4.q_ref.k_ref.v_ref.g_ref, bf16[4,2,384,21504]{3,2,1,0:T(8,128)(2,1)} %proj_in.4.q_ref.k_ref.v_ref.g_ref, bf16[4,2,384,21504]{3,2,1,0:T(8,128)(2,1)} %proj_in.4.q_ref.k_ref.v_ref.g_ref), custom_call_target="tpu_custom_call" | custom-call | flops 57982058496 | bytes 75497472 | tf_op jit(solution)/shard_map/attention/pallas_call | solution.py:199
  707.4 166.1 %proj_out.6.rest_0_ = bf16[4,2,384,3072]{3,2,1,0:T(8,128)(2,1)} custom-call(s32[1]{0:T(128)} %constant.53.clone.1.slot_ref, bf16[4,2,384,3072]{3,2,1,0:T(8,128)(2,1)} %attention.2.o_ref, bf16[4,2,384,21504]{3,2,1,0:T(8,128)(2,1)} %proj_in.4.q_ref.k_ref.v_ref.g_ref, bf16[2,15360,3072]{2,1,0:T(8,128)(2,1)} %w_ref.19, bf16[2,1,3072]{2,1,0:T(2,128)(2,1)} %copy.26.b_ref, ...), custom_call_target="tpu_custom_call" | custom-call | flops 144955146240 | bytes 188743680 | tf_op jit(solution)/shard_map/proj_out/pallas_call | solution.py:285
  873.5 166.2 %proj_out.7.x_ref = bf16[4,2,384,3072]{3,2,1,0:T(8,128)(2,1)} custom-call(s32[1]{0:T(128)} %constant.15.clone.1.slot_ref, bf16[4,2,384,3072]{3,2,1,0:T(8,128)(2,1)} %attention.2.o_ref, bf16[4,2,384,21504]{3,2,1,0:T(8,128)(2,1)} %proj_in.4.q_ref.k_ref.v_ref.g_ref, bf16[2,15360,3072]{2,1,0:T(8,128)(2,1)} %w_ref.19, ...), custom_call_target="tpu_custom_call", output_to_operand_aliasing={{}: (7, {})} | custom-call | flops 144955146240 | bytes 188743680 | tf_op jit(solution)/shard_map/proj_out/pallas_call | solution.py:285
  1039.8 484.8 %proj_in.5.q_ref.k_ref.v_ref.g_ref = bf16[4,2,384,21504]{3,2,1,0:T(8,128)(2,1)} custom-call(bf16[4,2,384,3072]{3,2,1,0:T(8,128)(2,1)} %proj_out.7.x_ref, f32[2,1,9216]{2,1,0:T(1,128)} %get-tuple-element.17.mod_ref, bf16[2,3072,21504]{2,1,0:T(8,128)(2,1)} %w_ref.15, bf16[2,1,21504]{2,1,0:T(2,128)(2,1)} %copy.23.b_ref, f32[2,1,128]{2,1,0:T(1,128)} %bitcast.32, ...), custom_call_target="tpu_custom_call" | custom-call | flops 405874409472 | bytes 660602880 | tf_op jit(solution)/shard_map/proj_in/pallas_call | solution.py:156
  1524.6 140.7 %attention.3.o_ref = bf16[4,2,384,3072]{3,2,1,0:T(8,128)(2,1)} custom-call(bf16[4,2,384,21504]{3,2,1,0:T(8,128)(2,1)} %proj_in.5.q_ref.k_ref.v_ref.g_ref, bf16[4,2,384,21504]{3,2,1,0:T(8,128)(2,1)} %proj_in.5.q_ref.k_ref.v_ref.g_ref, bf16[4,2,384,21504]{3,2,1,0:T(8,128)(2,1)} %proj_in.5.q_ref.k_ref.v_ref.g_ref), custom_call_target="tpu_custom_call" | custom-call | flops 57982058496 | bytes 75497472 | tf_op jit(solution)/shard_map/attention/pallas_call | solution.py:199
  1665.2 87.1 %proj_out.11 = bf16[1,2,384,3072]{3,2,1,0:T(8,128)(2,1)} custom-call(s32[1]{0:T(128)} %constant.53.clone.1.slot_ref, bf16[4,2,384,3072]{3,2,1,0:T(8,128)(2,1)} %attention.3.o_ref, bf16[4,2,384,21504]{3,2,1,0:T(8,128)(2,1)} %proj_in.5.q_ref.k_ref.v_ref.g_ref, bf16[2,15360,3072]{2,1,0:T(8,128)(2,1)} %w_ref.19, bf16[2,1,3072]{2,1,0:T(2,128)(2,1)} %copy.26.b_ref, ...), custom_call_target="tpu_custom_call" | custom-call | flops 72477573120 | bytes 94371840 | tf_op jit(solution)/shard_map/proj_out/pallas_call | solution.py:285
  1752.3 87.1 %proj_out.10 = bf16[1,2,384,3072]{3,2,1,0:T(8,128)(2,1)} custom-call(s32[1]{0:T(128)} %constant.53.clone.1.slot_ref, bf16[4,2,384,3072]{3,2,1,0:T(8,128)(2,1)} %attention.3.o_ref, bf16[4,2,384,21504]{3,2,1,0:T(8,128)(2,1)} %proj_in.5.q_ref.k_ref.v_ref.g_ref, bf16[2,15360,3072]{2,1,0:T(8,128)(2,1)} %w_ref.19, bf16[2,1,3072]{2,1,0:T(2,128)(2,1)} %copy.26.b_ref, ...), custom_call_target="tpu_custom_call" | custom-call | flops 72477573120 | bytes 94371840 | tf_op jit(solution)/shard_map/proj_out/pallas_call | solution.py:285
  1839.5 87.3 %proj_out.9 = bf16[1,2,384,3072]{3,2,1,0:T(8,128)(2,1)} custom-call(s32[1]{0:T(128)} %constant.53.clone.1.slot_ref, bf16[4,2,384,3072]{3,2,1,0:T(8,128)(2,1)} %attention.3.o_ref, bf16[4,2,384,21504]{3,2,1,0:T(8,128)(2,1)} %proj_in.5.q_ref.k_ref.v_ref.g_ref, bf16[2,15360,3072]{2,1,0:T(8,128)(2,1)} %w_ref.19, bf16[2,1,3072]{2,1,0:T(2,128)(2,1)} %copy.26.b_ref, ...), custom_call_target="tpu_custom_call" | custom-call | flops 72477573120 | bytes 94371840 | tf_op jit(solution)/shard_map/proj_out/pallas_call | solution.py:285
  1928.7 87.1 %proj_out.8 = bf16[4,2,384,3072]{3,2,1,0:T(8,128)(2,1)} custom-call(s32[1]{0:T(128)} %bitcast.me_ref.slot_ref, bf16[4,2,384,3072]{3,2,1,0:T(8,128)(2,1)} %attention.3.o_ref, bf16[4,2,384,21504]{3,2,1,0:T(8,128)(2,1)} %proj_in.5.q_ref.k_ref.v_ref.g_ref, bf16[2,15360,3072]{2,1,0:T(8,128)(2,1)} %w_ref.19, bf16[2,1,3072]{2,1,0:T(2,128)(2,1)} %copy.26.b_ref, ...), custom_call_target="tpu_custom_call" | custom-call | flops 72477573120 | bytes 94371840 | tf_op jit(solution)/shard_map/proj_out/pallas_call | solution.py:285
  2015.8 4.8 constant_dynamic-update-slice_fusion.4
  2020.6 111.7 %collective-permute-done.4 = bf16[1,2,384,3072]{3,2,1,0:T(8,128)(2,1)} collective-permute-done((bf16[1,2,384,3072]{3,2,1,0:T(8,128)(2,1)}, bf16[1,2,384,3072]{3,2,1,0:T(8,128)(2,1)}, u32[]{:S(2)}, u32[]{:S(2)}) %collective-permute-start.4) | collective-permute-done | bytes 4718624 | tf_op jit(solution)/shard_map/ppermute | solution.py:342
  2132.3 4.8 constant_dynamic-update-slice_fusion.3
  2137.2 4.8 constant_dynamic-update-slice_fusion.2
  (47 shorter events, 8.3 us)
Async XLA Ops:
  0.8 0.8 copy-start
  1.6 21.3 copy-start.3
  29.9 17.1 copy-start.1
  29.9 17.9 copy-start.4
  29.9 17.9 copy-start.5
  29.9 17.9 copy-start.2
  44.1 10.6 collective-permute-start.2
  44.1 265.6 %collective-permute-start = (bf16[1,2,384,3072]{3,2,1,0:T(8,128)(2,1)}, bf16[1,2,384,3072]{3,2,1,0:T(8,128)(2,1)}, u32[]{:S(2)}, u32[]{:S(2)}) collective-permute-start(bf16[1,2,384,3072]{3,2,1,0:T(8,128)(2,1)} %get-tuple-element.14), channel_id=1, source_target_pairs={{0,2},{1,3},{2,0},{3,1},{4,6},{5,7},{6,4},{7,5}} | collective-permute-start | bytes 14155784 | tf_op jit(solution)/shard_map/ppermute | solution.py:320
  45.9 268.6 %collective-permute-start.1 = (bf16[1,2,384,3072]{3,2,1,0:T(8,128)(2,1)}, bf16[1,2,384,3072]{3,2,1,0:T(8,128)(2,1)}, u32[]{:S(2)}, u32[]{:S(2)}) collective-permute-start(bf16[1,2,384,3072]{3,2,1,0:T(8,128)(2,1)} %get-tuple-element.13), channel_id=1, source_target_pairs={{0,3},{1,2},{2,1},{3,0},{4,7},{5,6},{6,5},{7,4}} | collective-permute-start | bytes 14155784 | tf_op jit(solution)/shard_map/ppermute | solution.py:320
  1926.8 210.4 %collective-permute-start.5 = (bf16[1,2,384,3072]{3,2,1,0:T(8,128)(2,1)}, bf16[1,2,384,3072]{3,2,1,0:T(8,128)(2,1)}, u32[]{:S(2)}, u32[]{:S(2)}) collective-permute-start(bf16[1,2,384,3072]{3,2,1,0:T(8,128)(2,1)} %proj_out.11), channel_id=1, source_target_pairs={{0,3},{1,2},{2,1},{3,0},{4,7},{5,6},{6,5},{7,4}} | collective-permute-start | bytes 14155784 | tf_op jit(solution)/shard_map/ppermute | solution.py:342
  1928.4 203.9 %collective-permute-start.4 = (bf16[1,2,384,3072]{3,2,1,0:T(8,128)(2,1)}, bf16[1,2,384,3072]{3,2,1,0:T(8,128)(2,1)}, u32[]{:S(2)}, u32[]{:S(2)}) collective-permute-start(bf16[1,2,384,3072]{3,2,1,0:T(8,128)(2,1)} %proj_out.10), channel_id=1, source_target_pairs={{0,2},{1,3},{2,0},{3,1},{4,6},{5,7},{6,4},{7,5}} | collective-permute-start | bytes 14155784 | tf_op jit(solution)/shard_map/ppermute | solution.py:342
  1928.7 87.1 %collective-permute-start.3 = (bf16[1,2,384,3072]{3,2,1,0:T(8,128)(2,1)}, bf16[1,2,384,3072]{3,2,1,0:T(8,128)(2,1)}, u32[]{:S(2)}, u32[]{:S(2)}) collective-permute-start(bf16[1,2,384,3072]{3,2,1,0:T(8,128)(2,1)} %proj_out.9), channel_id=1, source_target_pairs={{0,1},{1,0},{2,3},{3,2},{4,5},{5,4},{6,7},{7,6}} | collective-permute-start | bytes 14155784 | tf_op jit(solution)/shard_map/ppermute | solution.py:342
